TPU v7x, 32 devices: a whole 2x2x4 slice. The times are simulated.
32 devices in a mesh: dp: 16 (over z, y, x), mp: 2 (over core).
Axes of the slice: x: 2, y: 2, z: 4, core: 2. Of those that a mesh axis runs over, the one named last changes fastest.
Arguments:
- tokens: bfloat16 [32768, 768], P(('dp', 'mp')), may hold values from -6 to 6
- w_query: bfloat16 [768, 768], P('dp', 'mp'), may hold values from -0.625 to 0.625
- w_key: bfloat16 [768, 768], P('dp', 'mp'), may hold values from -0.625 to 0.625
- w_value: bfloat16 [768, 768], P('dp', 'mp'), may hold values from -0.21875 to 0.21875
- value_taps: float32 [12, 33], P('mp'), may hold values from -0.3 to 0.3
- w_output: bfloat16 [768, 768], P(None, ('dp', 'mp')), may hold values from -0.875 to 0.875
- first_gain: bfloat16 [768], P(('dp', 'mp')), may hold values from 0.25 to 1.75
- first_bias: bfloat16 [768], P(('dp', 'mp')), may hold values from -1.5 to 1.5
- w_expand: bfloat16 [768, 3072], P('dp', 'mp'), may hold values from -0.21875 to 0.21875
- w_shrink: bfloat16 [3072, 768], P('mp', 'dp'), may hold values from -0.21875 to 0.21875
- second_gain: bfloat16 [768], P(('dp', 'mp')), may hold values from 0.25 to 1.75
- second_bias: bfloat16 [768], P(('dp', 'mp')), may hold values from -1.5 to 1.5
- doc_lengths: int32 [32], replicated, may hold values from 256 to 1024, as said below
- out_grad: bfloat16 [32768, 768], P(('dp', 'mp')), may hold values from -6 to 6
Outputs:
- layer_out: bfloat16 [32768, 768], P(('dp', 'mp'))
- tokens_grad: float32 [32768, 768], P(('dp', 'mp'))
- query_grad: float32 [768, 768], P('dp', 'mp')
- key_grad: float32 [768, 768], P('dp', 'mp')
- value_grad: float32 [768, 768], P('dp', 'mp')
- taps_grad: float32 [12, 33], P('mp')
- output_grad: float32 [768, 768], P(None, ('dp', 'mp'))
- first_gain_grad: float32 [768], P(('dp', 'mp'))
- first_bias_grad: float32 [768], P(('dp', 'mp'))
- expand_grad: float32 [768, 3072], P('dp', 'mp')
- shrink_grad: float32 [3072, 768], P('mp', 'dp')
- second_gain_grad: float32 [768], P(('dp', 'mp'))
- second_bias_grad: float32 [768], P(('dp', 'mp'))
Inputs may be any that keep to these rules, and one draw needn't show every extreme that they name: Document i occupies the first doc_lengths[i] positions of slot i of 1024 positions; the rest is padding. In every draw some document fills its whole slot.
All inputs are finite; a program needn't handle non-finite values.
Results may differ from a plain program's by a relative error of at most 0.018.
The roundings to bfloat16 on the way count: a program that leaves them out, or rounds other values in their place, can miss the bound.
Values may be sent and summed in bfloat16 or wider, within the bound.
A program may use at most 320 MiB of HBM per device.

v0:
```python
import jax
import jax.numpy as jnp
from jax import lax
from jax.sharding import PartitionSpec as P

HEAD_DIM = 64
LANDMARKS = 64
KERNEL = 33
PINV_STEPS = 6
HIGH = lax.Precision.HIGHEST


def ahead(left, right):
    return jnp.dot(left, right, preferred_element_type=jnp.float32)


def against(left, right):
    return lax.dot_general(
        left, right, (((1,), (1,)), ((), ())), preferred_element_type=jnp.float32
    )


def across(left, right):
    return lax.dot_general(
        left, right, (((0,), (0,)), ((), ())), preferred_element_type=jnp.float32
    )


def layer_norm(values, gain, bias):
    middle = jnp.mean(values, axis=-1, keepdims=True)
    centered = values - middle
    variance = jnp.mean(centered * centered, axis=-1, keepdims=True)
    return centered * lax.rsqrt(variance + 1e-05) * gain + bias


def exact_gelu(values):
    return jax.nn.gelu(values, approximate=False)


def inverse_estimate(matrix):
    widest = jnp.max(jnp.sum(matrix, axis=-2), axis=-1)
    current = jnp.swapaxes(matrix, -1, -2) / widest[:, None, None]
    identity = jnp.eye(matrix.shape[-1], dtype=jnp.float32)[None]
    for step in range(PINV_STEPS):
        product = jnp.einsum("hij,hjk->hik", matrix, current, precision=HIGH)
        inner_term = 7.0 * identity - product
        inner_term = 15.0 * identity - jnp.einsum(
            "hij,hjk->hik", product, inner_term, precision=HIGH
        )
        inner_term = 13.0 * identity - jnp.einsum(
            "hij,hjk->hik", product, inner_term, precision=HIGH
        )
        current = 0.25 * jnp.einsum("hij,hjk->hik", current, inner_term, precision=HIGH)
    return current


def nystrom(query, keys, values, taps, length):
    slots = query.shape[0]
    positions = jnp.arange(slots, dtype=jnp.int32)
    valid = positions < length
    weight = valid.astype(jnp.float32)
    segment = positions * LANDMARKS // length
    member = (
        (segment[None, :] == jnp.arange(LANDMARKS, dtype=jnp.int32)[:, None]) & valid[None, :]
    ).astype(jnp.float32)
    member = member / jnp.sum(member, axis=1, keepdims=True)
    mark_query = jnp.einsum("js,shd->hjd", member, query, precision=HIGH)
    mark_keys = jnp.einsum("js,shd->hjd", member, keys, precision=HIGH)
    scale = HEAD_DIM ** (-0.5)
    first = jax.nn.softmax(
        jnp.einsum("shd,hjd->hsj", query, mark_keys, precision=HIGH) * scale, axis=-1
    )
    second = jax.nn.softmax(
        jnp.einsum("hid,hjd->hij", mark_query, mark_keys, precision=HIGH) * scale, axis=-1
    )
    third_scores = jnp.einsum("hjd,shd->hjs", mark_query, keys, precision=HIGH) * scale
    third = jax.nn.softmax(jnp.where(valid[None, None, :], third_scores, -1e30), axis=-1)
    inverse = inverse_estimate(second)
    summary = jnp.einsum("hjs,shd->hjd", third, values, precision=HIGH)
    carried = jnp.einsum("hij,hjd->hid", inverse, summary, precision=HIGH)
    mixed = jnp.einsum("hsj,hjd->shd", first, carried, precision=HIGH)
    radius = KERNEL // 2
    padded = jnp.pad(values * weight[:, None, None], ((radius, radius), (0, 0), (0, 0)))
    for index in range(KERNEL):
        mixed = mixed + taps[:, index][None, :, None] * padded[index : index + slots]
    mixed = mixed * weight[:, None, None]
    return mixed.reshape(slots, query.shape[1] * HEAD_DIM)


def on_device(
    tokens,
    w_query,
    w_key,
    w_value,
    value_taps,
    w_output,
    first_gain,
    first_bias,
    w_expand,
    w_shrink,
    second_gain,
    second_bias,
    doc_lengths,
    out_grad,
):
    parts = lax.axis_size("mp")
    group = lax.axis_index("dp")
    slots = tokens.shape[0]
    pair = lax.dynamic_slice_in_dim(doc_lengths, group * parts, parts)
    full_query, full_keys, full_values, full_expand, full_shrink = (
        lax.all_gather(w_query, "dp", axis=0, tiled=True),
        lax.all_gather(w_key, "dp", axis=0, tiled=True),
        lax.all_gather(w_value, "dp", axis=0, tiled=True),
        lax.all_gather(w_expand, "dp", axis=0, tiled=True),
        lax.all_gather(w_shrink, "dp", axis=1, tiled=True),
    )
    full_output, gain_one, bias_one, gain_two, bias_two = (
        lax.all_gather(w_output, ("dp", "mp"), axis=1, tiled=True),
        lax.all_gather(first_gain, ("dp", "mp"), axis=0, tiled=True),
        lax.all_gather(first_bias, ("dp", "mp"), axis=0, tiled=True),
        lax.all_gather(second_gain, ("dp", "mp"), axis=0, tiled=True),
        lax.all_gather(second_bias, ("dp", "mp"), axis=0, tiled=True),
    )
    gain_one = gain_one.astype(jnp.float32)
    bias_one = bias_one.astype(jnp.float32)
    gain_two = gain_two.astype(jnp.float32)
    bias_two = bias_two.astype(jnp.float32)
    local_heads = full_query.shape[1] // HEAD_DIM
    grouped = lax.all_gather(tokens, "mp", axis=0, tiled=True)
    query_low = ahead(grouped, full_query).astype(jnp.bfloat16)
    keys_low = ahead(grouped, full_keys).astype(jnp.bfloat16)
    values_low = ahead(grouped, full_values).astype(jnp.bfloat16)

    def attention_core(query, keys, values, taps):
        shape = (parts, slots, local_heads, HEAD_DIM)
        mixed = jax.vmap(nystrom, in_axes=(0, 0, 0, None, 0))(
            query.reshape(shape), keys.reshape(shape), values.reshape(shape), taps, pair
        )
        return mixed.reshape(parts * slots, local_heads * HEAD_DIM)

    attended, core_back = jax.vjp(
        attention_core,
        query_low.astype(jnp.float32),
        keys_low.astype(jnp.float32),
        values_low.astype(jnp.float32),
        value_taps,
    )
    attended_tok = lax.all_to_all(
        attended.astype(jnp.bfloat16), "mp", split_axis=0, concat_axis=1, tiled=True
    )
    projected = ahead(attended_tok, full_output)
    first_out, first_back = jax.vjp(
        layer_norm, tokens.astype(jnp.float32) + projected, gain_one, bias_one
    )
    hidden_all = lax.all_gather(first_out.astype(jnp.bfloat16), "mp", axis=0, tiled=True)
    pre = ahead(hidden_all, full_expand)
    active, gelu_back = jax.vjp(exact_gelu, pre)
    active_low = active.astype(jnp.bfloat16)
    branch = lax.psum_scatter(
        ahead(active_low, full_shrink).astype(jnp.bfloat16), "mp", scatter_dimension=0, tiled=True
    ).astype(jnp.float32)
    result, second_back = jax.vjp(layer_norm, first_out + branch, gain_two, bias_two)
    layer_out = result.astype(jnp.bfloat16)
    d_second_in, gain_two_grad, bias_two_grad = second_back(out_grad.astype(jnp.float32))
    branch_grad = lax.all_gather(d_second_in.astype(jnp.bfloat16), "mp", axis=0, tiled=True)
    back_query, back_keys, back_values, back_expand, back_shrink = (
        lax.all_gather(w_query, "dp", axis=0, tiled=True),
        lax.all_gather(w_key, "dp", axis=0, tiled=True),
        lax.all_gather(w_value, "dp", axis=0, tiled=True),
        lax.all_gather(w_expand, "dp", axis=0, tiled=True),
        lax.all_gather(w_shrink, "dp", axis=1, tiled=True),
    )
    (d_pre,) = gelu_back(against(branch_grad, back_shrink))
    d_pre_low = d_pre.astype(jnp.bfloat16)
    shrink_grad = across(active_low, branch_grad)
    expand_grad = across(hidden_all, d_pre_low)
    d_hidden = lax.psum_scatter(
        against(d_pre_low, back_expand).astype(jnp.bfloat16), "mp", scatter_dimension=0, tiled=True
    ).astype(jnp.float32)
    d_first_in, gain_one_grad, bias_one_grad = first_back(d_second_in + d_hidden)
    d_projected = d_first_in.astype(jnp.bfloat16)
    output_grad = across(attended_tok, d_projected)
    d_attended = against(d_projected, full_output).astype(jnp.bfloat16)
    d_heads = lax.all_to_all(d_attended, "mp", split_axis=1, concat_axis=0, tiled=True)
    d_query, d_keys, d_values, taps_grad = core_back(d_heads.astype(jnp.float32))
    d_query = d_query.astype(jnp.bfloat16)
    d_keys = d_keys.astype(jnp.bfloat16)
    d_values = d_values.astype(jnp.bfloat16)
    query_grad = across(grouped, d_query)
    key_grad = across(grouped, d_keys)
    value_grad = across(grouped, d_values)
    total = against(d_query, back_query)
    total = total + against(d_keys, back_keys)
    tokens_grad = d_first_in + lax.psum_scatter(
        (total + against(d_values, back_values)).astype(jnp.bfloat16),
        "mp",
        scatter_dimension=0,
        tiled=True,
    ).astype(jnp.float32)
    query_grad, key_grad, value_grad, expand_grad, shrink_grad = (
        lax.psum_scatter(query_grad, "dp", scatter_dimension=0, tiled=True),
        lax.psum_scatter(key_grad, "dp", scatter_dimension=0, tiled=True),
        lax.psum_scatter(value_grad, "dp", scatter_dimension=0, tiled=True),
        lax.psum_scatter(expand_grad, "dp", scatter_dimension=0, tiled=True),
        lax.psum_scatter(shrink_grad, "dp", scatter_dimension=1, tiled=True),
    )
    output_grad, gain_one_grad, bias_one_grad, gain_two_grad, bias_two_grad = (
        lax.psum_scatter(output_grad, ("dp", "mp"), scatter_dimension=1, tiled=True),
        lax.psum_scatter(gain_one_grad, ("dp", "mp"), scatter_dimension=0, tiled=True),
        lax.psum_scatter(bias_one_grad, ("dp", "mp"), scatter_dimension=0, tiled=True),
        lax.psum_scatter(gain_two_grad, ("dp", "mp"), scatter_dimension=0, tiled=True),
        lax.psum_scatter(bias_two_grad, ("dp", "mp"), scatter_dimension=0, tiled=True),
    )
    taps_grad = lax.psum(taps_grad, "dp")
    return (
        layer_out,
        tokens_grad,
        query_grad,
        key_grad,
        value_grad,
        taps_grad,
        output_grad,
        gain_one_grad,
        bias_one_grad,
        expand_grad,
        shrink_grad,
        gain_two_grad,
        bias_two_grad,
    )


def solution(mesh):
    in_specs = (
        P(("dp", "mp"), None),
        P("dp", "mp"),
        P("dp", "mp"),
        P("dp", "mp"),
        P("mp", None),
        P(None, ("dp", "mp")),
        P(("dp", "mp")),
        P(("dp", "mp")),
        P("dp", "mp"),
        P("mp", "dp"),
        P(("dp", "mp")),
        P(("dp", "mp")),
        P(),
        P(("dp", "mp"), None),
    )
    out_specs = (
        P(("dp", "mp"), None),
        P(("dp", "mp"), None),
        P("dp", "mp"),
        P("dp", "mp"),
        P("dp", "mp"),
        P("mp", None),
        P(None, ("dp", "mp")),
        P(("dp", "mp")),
        P(("dp", "mp")),
        P("dp", "mp"),
        P("mp", "dp"),
        P(("dp", "mp")),
        P(("dp", "mp")),
    )
    return jax.shard_map(
        on_device, mesh=mesh, in_specs=in_specs, out_specs=out_specs, check_vma=False
    )
```

profile of v0, /device:TPU:0, one launch (start us, length us, event | category | flops | bytes accessed | tf_op | source)
XLA Modules:
  0.0 1484.3 jit_solution(6945524106746862283)
XLA Ops:
  18.9 42.1 %all-reduce.76 = (bf16[768]{0:T(1024)(128)(2,1)S(1)}, bf16[768]{0:T(1024)(128)(2,1)S(1)}, bf16[768]{0:T(1024)(128)(2,1)}, bf16[768]{0:T(1024)(128)(2,1)}) all-reduce(bf16[768]{0:T(1024)(128)(2,1)S(1)} %dynamic-update-slice.1, bf16[768]{0:T(1024)(128)(2,1)S(1)} %dynamic-update-slice, ...), channel_id=1, replica_groups=mesh['dp'=16,'mp'=2] {'dp','mp'}, use_global_device_ids=true, to_apply=%add.68 | all-reduce | flops 3072 | bytes 12288
  62.4 44.0 %all_gather.45 = bf16[768,384]{1,0:T(8,128)(2,1)S(1)} all-gather(bf16[48,384]{1,0:T(8,128)(2,1)S(1)} %copy-done.119), channel_id=1, replica_groups=mesh['dp'=16,'mp'=2] {'dp'}, dimensions={0}, use_global_device_ids=true | all-gather | bytes 626688 | tf_op jit(solution)/shard_map/all_gather | solution.py:111
  106.3 41.1 %all_gather.46 = bf16[768,384]{1,0:T(8,128)(2,1)S(1)} all-gather(bf16[48,384]{1,0:T(8,128)(2,1)S(1)} %copy-done.120), channel_id=1, replica_groups=mesh['dp'=16,'mp'=2] {'dp'}, dimensions={0}, use_global_device_ids=true | all-gather | bytes 626688 | tf_op jit(solution)/shard_map/all_gather | solution.py:112
  147.4 43.7 %all_gather.47 = bf16[768,384]{1,0:T(8,128)(2,1)} all-gather(bf16[48,384]{1,0:T(8,128)(2,1)S(1)} %copy-done.121), channel_id=1, replica_groups=mesh['dp'=16,'mp'=2] {'dp'}, dimensions={0}, use_global_device_ids=true | all-gather | bytes 626688 | tf_op jit(solution)/shard_map/all_gather | solution.py:113
  267.9 29.7 %multiply_convert_fusion.1 = bf16[2,1024,6,64]{1,3,2,0:T(8,128)(2,1)} fusion(f32[2,1024,6,64]{1,3,2,0:T(8,128)S(1)} %copy_multiply_fusion, f32[2,6,64,64]{3,2,1,0:T(8,128)S(1)} %fusion.157, f32[6]{0:T(128)S(1)} %copy-done.146, f32[6]{0:T(128)S(1)} %copy-done.156, f32[6]{0:T(128)S(1)} %copy-done.158, f32[6]{0:T(128)S(1)} %copy-done.160, ...), kind=kOutput, calls=%fused_computation.121 | convolution fusion | flops 659816448 | bytes 8168216 | tf_op jit(solution)/shard_map/jvp(vmap(hsj,hjd->shd))/dot_general | solution.py:81
  319.1 35.5 %multiply_convert_fusion = (bf16[2048,1536]{1,0:T(8,128)(2,1)}, f32[2048,1536]{1,0:T(8,128)}, f32[2048,1536]{1,0:T(8,128)}) fusion(bf16[2048,768]{0,1:T(8,128)(2,1)} %all-gather.11.cloned.1.call-done, bf16[768,1536]{1,0:T(8,128)(2,1)} %all-gather.13.cloned.1.call-done), kind=kOutput, calls=%fused_computation.3 | convolution fusion | flops 5036310528 | bytes 36962304 | tf_op jit(solution)/shard_map/dot_general | solution.py:14
  354.6 30.5 %all-gather.15.cloned.1.call-done = bf16[1536,768]{0,1:T(8,128)(2,1)} async-done(((bf16[1536,48]{0,1:T(8,128)(2,1)}), bf16[1536,768]{0,1:T(8,128)(2,1)}) %all-gather.15.cloned.1.call-update) | async-done | bytes 2359312 | tf_op jit(solution)/shard_map/all_gather | solution.py:115
  415.1 13.5 all-gather.17.cloned.1.call-done
  428.6 17.3 %add_convert_fusion = bf16[2048,1536]{1,0:T(8,128)(2,1)S(1)} fusion(f32[2048,1536]{1,0:T(8,128)} %get-tuple-element.153, f32[2048,1536]{1,0:T(8,128)} %get-tuple-element.200, bf16[2048,768]{0,1:T(8,128)(2,1)} %all-gather.17.cloned.1.call-done, bf16[1536,768]{0,1:T(8,128)(2,1)} %all-gather.15.cloned.1.call-done), kind=kOutput, calls=%fused_computation.2 | convolution fusion | flops 4875878400 | bytes 36962304 | tf_op jit(solution)/shard_map/dot_general | solution.py:18
  534.2 15.2 %multiply_reduce_fusion.32 = (f32[6]{0:T(128)}, f32[6]{0:T(128)}, f32[6]{0:T(128)}, f32[6]{0:T(128)}, f32[6]{0:T(128)}, /*index=5*/f32[6]{0:T(128)}, f32[6]{0:T(...) fusion(f32[2,1024,6,64]{1,3,2,0:T(8,128)S(1)} %copy-done.5, ...), kind=kLoop, calls=%fused_computation.107 | loop fusion | flops 25952166 | bytes 12591512 | tf_op jit(solution)/shard_map/transpose(jvp(vmap()))/reduce_sum | solution.py:85
  549.6 16.9 %broadcast_multiply_fusion.1 = (f32[2,1024,6,64]{1,3,2,0:T(8,128)}, f32[2,1024,6,64]{1,3,2,0:T(8,128)}, f32[2,1024,6,64]{1,3,2,0:T(8,128)}, f32[2,1024,6,64]{1,3...) fusion(f32[6]{0:T(128)S(1)} %copy-done.157, ...), kind=kLoop, calls=%fused_computation.168 | loop fusion | flops 11796480 | bytes 47194448 | tf_op jit(solution)/shard_map/transpose(jvp(vmap()))/mul | solution.py:85
  566.5 21.3 %broadcast_multiply_fusion = (f32[2,1024,6,64]{1,3,2,0:T(8,128)}, f32[2,1024,6,64]{1,3,2,0:T(8,128)}, f32[2,1024,6,64]{1,3,2,0:T(8,128)}, f32[2,1024,6,64]{1,3,2...) fusion(f32[6]{0:T(128)} %get-tuple-element.134, ...), kind=kLoop, calls=%fused_computation.167 | loop fusion | flops 14155776 | bytes 56631704 | tf_op jit(solution)/shard_map/transpose(jvp(vmap()))/mul | solution.py:85
  630.5 34.7 %pad_add_fusion = f32[2,1056,6,64]{1,3,2,0:T(8,128)} fusion(f32[2,1024,6,64]{1,3,2,0:T(8,128)} %get-tuple-element.163, f32[2,1024,6,64]{1,3,2,0:T(8,128)} %get-tuple-element.164, f32[2,1024,6,64]{1,3,2,0:T(8,128)} %get-tuple-element.165, f32[2,1024,6,64]{1,3,2,0:T(8,128)} %get-tuple-element.166, f32[2,1024,6,64]{1,3,2,0:T(8,128)} %get-tuple-element.167, ...), kind=kLoop, calls=%fused_computation.25 | loop fusion | flops 21086208 | bytes 88178688 | tf_op jit(solution)/shard_map/transpose(jvp(vmap()))/add_any | solution.py:85
  665.2 12.1 fusion.12
  712.2 9.6 fusion.175
  721.8 9.7 fusion.172
  734.2 40.9 %all-reduce.75 = (f32[768]{0:T(1024)S(1)}, f32[768]{0:T(1024)S(1)}, f32[768]{0:T(1024)S(1)}, f32[768]{0:T(1024)S(1)}) all-reduce(f32[768]{0:T(1024)S(1)} %copy-done.126, f32[768]{0:T(1024)S(1)} %copy-done.127, f32[768]{0:T(1024)S(1)} %copy-done.124, f32[768]{0:T(1024)S(1)} %copy-done.125), channel_id=9, replica_groups=mesh['dp'=16,'mp'=2] {'dp','mp'}, use_global_device_ids=true, to_apply=%region_65.66.clone | all-reduce | flops 3072 | bytes 24576
  780.4 28.5 %multiply_reduce_fusion.33 = (f32[6]{0:T(128)S(1)}, f32[6]{0:T(128)S(1)}, f32[6]{0:T(128)S(1)}, f32[6]{0:T(128)S(1)}, f32[6]{0:T(128)S(1)}, /*index=5*/f32[6]{0:...) fusion(f32[2,1024,6,64]{1,3,2,0:T(8,128)} %copy-done.4, ...), kind=kLoop, calls=%fused_computation.108 | loop fusion | flops 27525018 | bytes 6300056 | tf_op jit(solution)/shard_map/transpose(jvp(vmap()))/reduce_sum | solution.py:85
  809.1 75.8 %psum.7 = f32[6,33]{0,1:T(8,128)S(1)} all-reduce(f32[6,33]{0,1:T(8,128)S(1)} %pad_add_fusion.7), channel_id=1, replica_groups=mesh['dp'=16,'mp'=2] {'dp'}, use_global_device_ids=true, to_apply=%region_62.63 | all-reduce | flops 198 | bytes 1584 | tf_op jit(solution)/shard_map/psum | solution.py:214
  890.8 66.8 %reduce-scatter.30.cloned.1.call-done = f32[48,384]{1,0:T(8,128)} async-done(((f32[768,384]{1,0:T(8,128)}), f32[48,384]{1,0:T(8,128)}) %reduce-scatter.30.cloned.1.call-update) | async-done | bytes 73744
  957.6 129.3 %reduce-scatter.32.cloned.1.call-done = f32[48,384]{1,0:T(8,128)} async-done(((f32[768,384]{1,0:T(8,128)}), f32[48,384]{1,0:T(8,128)}) %reduce-scatter.32.cloned.1.call-update) | async-done | bytes 73744
  1086.9 104.5 %reduce-scatter.22.cloned.1.call-done = f32[768,24]{0,1:T(8,128)} async-done(((f32[768,768]{0,1:T(8,128)}), f32[768,24]{0,1:T(8,128)}) %reduce-scatter.22.cloned.1.call-update) | async-done | bytes 73744 | tf_op jit(solution)/shard_map/reduce_scatter | solution.py:208
  1191.3 143.0 %reduce-scatter.26.cloned.1.call-done = f32[1536,48]{0,1:T(8,128)} async-done(((f32[1536,768]{0,1:T(8,128)}), f32[1536,48]{0,1:T(8,128)}) %reduce-scatter.26.cloned.1.call-update) | async-done | bytes 294928 | tf_op jit(solution)/shard_map/reduce_scatter | solution.py:205
  1334.3 143.3 %reduce-scatter.24.cloned.1.call-done = f32[48,1536]{1,0:T(8,128)} async-done(((f32[768,1536]{1,0:T(8,128)}), f32[48,1536]{1,0:T(8,128)}) %reduce-scatter.24.cloned.1.call-update) | async-done | bytes 294928 | tf_op jit(solution)/shard_map/reduce_scatter | solution.py:204
  (675 shorter events, 317.5 us)
Async XLA Ops:
  7.2 55.0 %copy-start.204 = (s32[32]{0:T(128)S(1)}, s32[32]{0:T(128)}, u32[]{:S(2)}) copy-start(s32[32]{0:T(128)} %param.26) | copy-start | bytes 388
  7.2 55.1 %copy-start.119 = (bf16[48,384]{1,0:T(8,128)(2,1)S(1)}, bf16[48,384]{1,0:T(8,128)(2,1)}, u32[]{:S(2)}) copy-start(bf16[48,384]{1,0:T(8,128)(2,1)} %param.15) | copy-start | bytes 110596
  7.2 99.1 %copy-start.120 = (bf16[48,384]{1,0:T(8,128)(2,1)S(1)}, bf16[48,384]{1,0:T(8,128)(2,1)}, u32[]{:S(2)}) copy-start(bf16[48,384]{1,0:T(8,128)(2,1)} %param.16) | copy-start | bytes 110596
  7.3 140.2 %copy-start.121 = (bf16[48,384]{1,0:T(8,128)(2,1)S(1)}, bf16[48,384]{1,0:T(8,128)(2,1)}, u32[]{:S(2)}) copy-start(bf16[48,384]{1,0:T(8,128)(2,1)} %param.17) | copy-start | bytes 110596
  7.3 184.5 %all-gather.7.cloned.1.call-start = ((), (), s32[]{:S(2)}) async-start(), calls=%async_computation.11 | async-start | bytes 4718592 | tf_op jit(solution)/shard_map/all_gather | solution.py:129
  8.0 293.3 %all-gather.9.cloned.1.call-start = ((), (), s32[]{:S(2)}) async-start(), calls=%async_computation.12 | async-start | bytes 1216512 | tf_op jit(solution)/shard_map/all_gather | solution.py:118
  8.7 302.8 %all-gather.13.cloned.1.call-start = ((), (), s32[]{:S(2)}) async-start(), calls=%async_computation.14 | async-start | bytes 2506752 | tf_op jit(solution)/shard_map/all_gather | solution.py:114
  62.3 151.3 %copy-start.102 = (pred[2,1024]{1,0:T(4,128)(4,1)}, pred[2,1024]{1,0:T(4,128)(4,1)S(1)}, u32[]{:S(2)}) copy-start(pred[2,1024]{1,0:T(4,128)(4,1)S(1)} %get-tuple-element.190) | copy-start | bytes 6148
  62.4 204.7 %copy-start.94 = (f32[2,1024]{1,0:T(2,128)}, f32[2,1024]{1,0:T(2,128)S(1)}, u32[]{:S(2)}) copy-start(f32[2,1024]{1,0:T(2,128)S(1)} %get-tuple-element.191) | copy-start | bytes 24580
  106.3 94.6 %copy-start.75 = (bf16[768,384]{1,0:T(8,128)(2,1)}, bf16[768,384]{1,0:T(8,128)(2,1)S(1)}, u32[]{:S(2)}) copy-start(bf16[768,384]{1,0:T(8,128)(2,1)S(1)} %all_gather.45) | copy-start | bytes 1769476
  147.4 44.4 %copy-start.77 = (bf16[768,384]{1,0:T(8,128)(2,1)}, bf16[768,384]{1,0:T(8,128)(2,1)S(1)}, u32[]{:S(2)}) copy-start(bf16[768,384]{1,0:T(8,128)(2,1)S(1)} %all_gather.46) | copy-start | bytes 1769476
  297.5 6.2 all-to-all-start
  301.2 17.8 %all-gather.11.cloned.1.call-start = ((), (), s32[]{:S(2)}) async-start(), calls=%async_computation.13 | async-start | bytes 4718592 | tf_op jit(solution)/shard_map/all_gather | solution.py:155
  310.9 74.2 %all-gather.15.cloned.1.call-start = ((), (), s32[]{:S(2)}) async-start(), calls=%async_computation.15 | async-start | bytes 2506752 | tf_op jit(solution)/shard_map/all_gather | solution.py:115
  311.5 92.2 %reduce-scatter.16.cloned.1.call-start = ((), (), s32[]{:S(2)}) async-start(), calls=%async_computation.16 | async-start | bytes 4718592 | tf_op jit(solution)/shard_map/reduce_scatter | solution.py:159
  394.2 34.4 %all-gather.17.cloned.1.call-start = ((), (), s32[]{:S(2)}) async-start(), calls=%async_computation.17 | async-start | bytes 4718592 | tf_op jit(solution)/shard_map/all_gather | solution.py:165
  415.1 52.3 %reduce-scatter.18.cloned.1.call-start = ((), (), s32[]{:S(2)}) async-start(), calls=%async_computation.18 | async-start | bytes 4718592 | tf_op jit(solution)/shard_map/reduce_scatter | solution.py:177
  455.1 430.5 %reduce-scatter.20.cloned.1.call-start = ((), (), s32[]{:S(2)}) async-start(), calls=%async_computation.19 | async-start | bytes 4718592 | tf_op jit(solution)/shard_map/reduce_scatter | solution.py:194
  684.1 206.7 %reduce-scatter.28.cloned.1.call-start = ((), (), s32[]{:S(2)}) async-start(), calls=%async_computation.23 | async-start | bytes 1253376
  691.6 266.0 %reduce-scatter.30.cloned.1.call-start = ((), (), s32[]{:S(2)}) async-start(), calls=%async_computation.24 | async-start | bytes 1253376
  699.4 387.5 %reduce-scatter.32.cloned.1.call-start = ((), (), s32[]{:S(2)}) async-start(), calls=%async_computation.25 | async-start | bytes 1253376
  706.9 484.5 %reduce-scatter.22.cloned.1.call-start = ((), (), s32[]{:S(2)}) async-start(), calls=%async_computation.20 | async-start | bytes 2433024 | tf_op jit(solution)/shard_map/reduce_scatter | solution.py:208
  712.1 622.2 %reduce-scatter.26.cloned.1.call-start = ((), (), s32[]{:S(2)}) async-start(), calls=%async_computation.22 | async-start | bytes 5013504 | tf_op jit(solution)/shard_map/reduce_scatter | solution.py:205
  721.8 755.8 %reduce-scatter.24.cloned.1.call-start = ((), (), s32[]{:S(2)}) async-start(), calls=%async_computation.21 | async-start | bytes 5013504 | tf_op jit(solution)/shard_map/reduce_scatter | solution.py:204
  (211 other events, 1433.2 us)
Sparse Core Ops, SparseCore 0:
  9.6 14.8 all-gather.6
  27.4 56.4 all-gather.8
  86.7 69.3 all-gather.12
  311.0 8.0 all-gather.10
  321.7 63.3 all-gather.14
  394.3 9.3 reduce-scatter.15
  415.2 13.3 all-gather.16
  455.2 12.1 reduce-scatter.17
  684.2 12.2 reduce-scatter.19
  701.7 126.3 reduce-scatter.27
  833.4 124.1 reduce-scatter.29
  962.8 124.0 reduce-scatter.31
  1092.7 98.5 reduce-scatter.21
  1196.9 137.3 reduce-scatter.25
  1339.9 137.6 reduce-scatter.23
where the time goes:
time: 1490 us; the launch traced here: 1480 us
  waiting for transfers between devices  658 us (44%)
  blocking collectives  293 us (20%)
  matrix products  288 us (19%)
  other arithmetic  154 us (10%)
  local copies, waits for them, and re-layouts  70.2 us (5%)
  between operations  17.8 us (1%)
    unnamed x18, waiting for transfers between devices  199 us
    reduce_scatter x1, waiting for transfers between devices, on_device(): lax.psum_scatter(expand_grad, 'dp', scatter_dimension=0, tiled=True)  143 us
    reduce_scatter x1, waiting for transfers between devices, on_device(): lax.psum_scatter(shrink_grad, 'dp', scatter_dimension=1, tiled=True)  143 us
    reduce_scatter x1, waiting for transfers between devices, on_device(): lax.psum_scatter(output_grad, ('dp', 'mp'), scatter_dimension=1, tiled=True)  104 us
    unnamed x2, blocking collectives  83 us
    psum x1, blocking collectives, on_device(): taps_grad = lax.psum(taps_grad, 'dp')  75.8 us
    dot_general x6, matrix products, ahead(): return jnp.dot(left, right, preferred_element_type=jnp.float32)  60.9 us
    reduce_sum x4, other arithmetic, nystrom(): mixed = mixed + taps[:, index][None, :, None] * padded[index:index + slots]  46.4 us
  transfers between devices with their start and end apart: 16, of which 11 were waited for; matrix products, arithmetic and copies ran while one was open for 17% of the time, Pallas kernels for 0%

commit v1 on v0

--- a/solution.py
+++ b/solution.py
@@ -211,7 +211,11 @@
         lax.psum_scatter(gain_two_grad, ("dp", "mp"), scatter_dimension=0, tiled=True),
         lax.psum_scatter(bias_two_grad, ("dp", "mp"), scatter_dimension=0, tiled=True),
     )
-    taps_grad = lax.psum(taps_grad, "dp")
+    taps_grad = taps_grad
+    for hop in (1, 2, 4, 8):
+        taps_grad = taps_grad + lax.ppermute(
+            taps_grad, "dp", [(dev, dev ^ hop) for dev in range(16)]
+        )
     return (
         layer_out,
         tokens_grad,

time: 1490 us -> 1490 us (level)
  blocking collectives: 293 us -> 216 us
  waiting for transfers between devices: 658 us -> 726 us
    psum x1 -> x0, blocking collectives: 75.8 us -> none  [on_device(): taps_grad = lax.psum(taps_grad, 'dp')]
    unnamed x18, waiting for transfers between devices: 199 us -> 263 us
    unnamed x461 -> x457, local copies, waits for them, and re-layouts: 37.1 us -> 37.2 us
  transfers between devices with their start and end apart: 16 -> 20, of which waited for: 11 -> 14; matrix products, arithmetic and copies ran while one was open for 17% -> 17% of each run, Pallas kernels for 0% -> 0%
where the time goes in v1:
time: 1490 us; the launch traced here: 1480 us
  waiting for transfers between devices  726 us (49%)
  matrix products  288 us (19%)
  blocking collectives  216 us (14%)
  other arithmetic  154 us (10%)
  local copies, waits for them, and re-layouts  70.3 us (5%)
  between operations  17.8 us (1%)
    unnamed x18, waiting for transfers between devices  263 us
    reduce_scatter x1, waiting for transfers between devices, on_device(): lax.psum_scatter(expand_grad, 'dp', scatter_dimension=0, tiled=True)  143 us
    reduce_scatter x1, waiting for transfers between devices, on_device(): lax.psum_scatter(shrink_grad, 'dp', scatter_dimension=1, tiled=True)  143 us
    reduce_scatter x1, waiting for transfers between devices, on_device(): lax.psum_scatter(output_grad, ('dp', 'mp'), scatter_dimension=1, tiled=True)  104 us
    unnamed x2, blocking collectives  82.2 us
    dot_general x6, matrix products, ahead(): return jnp.dot(left, right, preferred_element_type=jnp.float32)  60.8 us
    reduce_sum x4, other arithmetic, nystrom(): mixed = mixed + taps[:, index][None, :, None] * padded[index:index + slots]  46.4 us
    all_gather x1, blocking collectives, on_device(): lax.all_gather(w_query, 'dp', axis=0, tiled=True)  44 us
  transfers between devices with their start and end apart: 20, of which 14 were waited for; matrix products, arithmetic and copies ran while one was open for 17% of the time, Pallas kernels for 0%

profile of v1, /device:TPU:0, one launch (start us, length us, event | category | flops | bytes accessed | tf_op | source)
XLA Modules:
  0.0 1484.3 jit_solution(14730702727978279022)
XLA Ops:
  18.9 42.1 %all-reduce.76 = (bf16[768]{0:T(1024)(128)(2,1)S(1)}, bf16[768]{0:T(1024)(128)(2,1)S(1)}, bf16[768]{0:T(1024)(128)(2,1)}, bf16[768]{0:T(1024)(128)(2,1)}) all-reduce(bf16[768]{0:T(1024)(128)(2,1)S(1)} %dynamic-update-slice.1, bf16[768]{0:T(1024)(128)(2,1)S(1)} %dynamic-update-slice, ...), channel_id=1, replica_groups=mesh['dp'=16,'mp'=2] {'dp','mp'}, use_global_device_ids=true, to_apply=%add.68 | all-reduce | flops 3072 | bytes 12288
  62.4 44.0 %all_gather.45 = bf16[768,384]{1,0:T(8,128)(2,1)S(1)} all-gather(bf16[48,384]{1,0:T(8,128)(2,1)S(1)} %copy-done.119), channel_id=1, replica_groups=mesh['dp'=16,'mp'=2] {'dp'}, dimensions={0}, use_global_device_ids=true | all-gather | bytes 626688 | tf_op jit(solution)/shard_map/all_gather | solution.py:111
  106.4 41.2 %all_gather.46 = bf16[768,384]{1,0:T(8,128)(2,1)S(1)} all-gather(bf16[48,384]{1,0:T(8,128)(2,1)S(1)} %copy-done.120), channel_id=1, replica_groups=mesh['dp'=16,'mp'=2] {'dp'}, dimensions={0}, use_global_device_ids=true | all-gather | bytes 626688 | tf_op jit(solution)/shard_map/all_gather | solution.py:112
  147.6 43.8 %all_gather.47 = bf16[768,384]{1,0:T(8,128)(2,1)} all-gather(bf16[48,384]{1,0:T(8,128)(2,1)S(1)} %copy-done.121), channel_id=1, replica_groups=mesh['dp'=16,'mp'=2] {'dp'}, dimensions={0}, use_global_device_ids=true | all-gather | bytes 626688 | tf_op jit(solution)/shard_map/all_gather | solution.py:113
  268.0 29.7 %multiply_convert_fusion.1 = bf16[2,1024,6,64]{1,3,2,0:T(8,128)(2,1)} fusion(f32[2,1024,6,64]{1,3,2,0:T(8,128)S(1)} %copy_multiply_fusion, f32[2,6,64,64]{3,2,1,0:T(8,128)S(1)} %fusion.157, f32[6]{0:T(128)S(1)} %copy-done.159, f32[6]{0:T(128)S(1)} %copy-done.169, f32[6]{0:T(128)S(1)} %copy-done.171, f32[6]{0:T(128)S(1)} %copy-done.173, ...), kind=kOutput, calls=%fused_computation.121 | convolution fusion | flops 659816448 | bytes 8168216 | tf_op jit(solution)/shard_map/jvp(vmap(hsj,hjd->shd))/dot_general | solution.py:81
  319.1 35.5 %multiply_convert_fusion = (bf16[2048,1536]{1,0:T(8,128)(2,1)}, f32[2048,1536]{1,0:T(8,128)}, f32[2048,1536]{1,0:T(8,128)}) fusion(bf16[2048,768]{0,1:T(8,128)(2,1)} %all-gather.11.cloned.1.call-done, bf16[768,1536]{1,0:T(8,128)(2,1)} %all-gather.13.cloned.1.call-done), kind=kOutput, calls=%fused_computation.3 | convolution fusion | flops 5036310528 | bytes 36962304 | tf_op jit(solution)/shard_map/dot_general | solution.py:14
  354.6 30.5 %all-gather.15.cloned.1.call-done = bf16[1536,768]{0,1:T(8,128)(2,1)} async-done(((bf16[1536,48]{0,1:T(8,128)(2,1)}), bf16[1536,768]{0,1:T(8,128)(2,1)}) %all-gather.15.cloned.1.call-update) | async-done | bytes 2359312 | tf_op jit(solution)/shard_map/all_gather | solution.py:115
  385.2 9.0 convolution_convert_fusion.1
  415.1 13.5 all-gather.17.cloned.1.call-done
  428.6 17.3 %add_convert_fusion = bf16[2048,1536]{1,0:T(8,128)(2,1)S(1)} fusion(f32[2048,1536]{1,0:T(8,128)} %get-tuple-element.153, f32[2048,1536]{1,0:T(8,128)} %get-tuple-element.200, bf16[2048,768]{0,1:T(8,128)(2,1)} %all-gather.17.cloned.1.call-done, bf16[1536,768]{0,1:T(8,128)(2,1)} %all-gather.15.cloned.1.call-done), kind=kOutput, calls=%fused_computation.2 | convolution fusion | flops 4875878400 | bytes 36962304 | tf_op jit(solution)/shard_map/dot_general | solution.py:18
  534.2 15.2 %multiply_reduce_fusion.32 = (f32[6]{0:T(128)S(1)}, f32[6]{0:T(128)}, f32[6]{0:T(128)}, f32[6]{0:T(128)}, f32[6]{0:T(128)}, /*index=5*/f32[6]{0:T(128)}, f32[6]{...) fusion(f32[2,1024,6,64]{1,3,2,0:T(8,128)S(1)} %copy-done.5, ...), kind=kLoop, calls=%fused_computation.107 | loop fusion | flops 25952166 | bytes 12591512 | tf_op jit(solution)/shard_map/transpose(jvp(vmap()))/reduce_sum | solution.py:85
  549.5 16.9 %broadcast_multiply_fusion.1 = (f32[2,1024,6,64]{1,3,2,0:T(8,128)}, f32[2,1024,6,64]{1,3,2,0:T(8,128)}, f32[2,1024,6,64]{1,3,2,0:T(8,128)}, f32[2,1024,6,64]{1,3...) fusion(f32[6]{0:T(128)S(1)} %copy-done.170, ...), kind=kLoop, calls=%fused_computation.168 | loop fusion | flops 11796480 | bytes 47194448 | tf_op jit(solution)/shard_map/transpose(jvp(vmap()))/mul | solution.py:85
  566.4 21.3 %broadcast_multiply_fusion = (f32[2,1024,6,64]{1,3,2,0:T(8,128)}, f32[2,1024,6,64]{1,3,2,0:T(8,128)}, f32[2,1024,6,64]{1,3,2,0:T(8,128)}, f32[2,1024,6,64]{1,3,2...) fusion(f32[6]{0:T(128)} %get-tuple-element.134, ...), kind=kLoop, calls=%fused_computation.167 | loop fusion | flops 14155776 | bytes 56631704 | tf_op jit(solution)/shard_map/transpose(jvp(vmap()))/mul | solution.py:85
  630.4 34.7 %pad_add_fusion = f32[2,1056,6,64]{1,3,2,0:T(8,128)} fusion(f32[2,1024,6,64]{1,3,2,0:T(8,128)} %get-tuple-element.163, f32[2,1024,6,64]{1,3,2,0:T(8,128)} %get-tuple-element.164, f32[2,1024,6,64]{1,3,2,0:T(8,128)} %get-tuple-element.165, f32[2,1024,6,64]{1,3,2,0:T(8,128)} %get-tuple-element.166, f32[2,1024,6,64]{1,3,2,0:T(8,128)} %get-tuple-element.167, ...), kind=kLoop, calls=%fused_computation.25 | loop fusion | flops 21086208 | bytes 88178688 | tf_op jit(solution)/shard_map/transpose(jvp(vmap()))/add_any | solution.py:85
  665.2 12.1 fusion.12
  712.3 9.6 fusion.175
  721.9 9.7 fusion.172
  734.6 28.5 %multiply_reduce_fusion.33 = (f32[6]{0:T(128)S(1)}, f32[6]{0:T(128)S(1)}, f32[6]{0:T(128)S(1)}, f32[6]{0:T(128)S(1)}, f32[6]{0:T(128)S(1)}, /*index=5*/f32[6]{0:...) fusion(f32[2,1024,6,64]{1,3,2,0:T(8,128)} %copy-done.4, ...), kind=kLoop, calls=%fused_computation.108 | loop fusion | flops 27525018 | bytes 6300056 | tf_op jit(solution)/shard_map/transpose(jvp(vmap()))/reduce_sum | solution.py:85
  778.2 40.1 %all-reduce.75 = (f32[768]{0:T(1024)S(1)}, f32[768]{0:T(1024)S(1)}, f32[768]{0:T(1024)S(1)}, f32[768]{0:T(1024)S(1)}) all-reduce(f32[768]{0:T(1024)S(1)} %copy-done.126, f32[768]{0:T(1024)S(1)} %copy-done.127, f32[768]{0:T(1024)S(1)} %copy-done.124, f32[768]{0:T(1024)S(1)} %copy-done.125), channel_id=9, replica_groups=mesh['dp'=16,'mp'=2] {'dp','mp'}, use_global_device_ids=true, to_apply=%region_64.65.clone | all-reduce | flops 3072 | bytes 24576
  828.1 129.4 %reduce-scatter.30.cloned.1.call-done = f32[48,384]{1,0:T(8,128)} async-done(((f32[768,384]{1,0:T(8,128)}), f32[48,384]{1,0:T(8,128)}) %reduce-scatter.30.cloned.1.call-update) | async-done | bytes 73744
  957.5 129.2 %reduce-scatter.32.cloned.1.call-done = f32[48,384]{1,0:T(8,128)} async-done(((f32[768,384]{1,0:T(8,128)}), f32[48,384]{1,0:T(8,128)}) %reduce-scatter.32.cloned.1.call-update) | async-done | bytes 73744
  1086.7 104.5 %reduce-scatter.22.cloned.1.call-done = f32[768,24]{0,1:T(8,128)} async-done(((f32[768,768]{0,1:T(8,128)}), f32[768,24]{0,1:T(8,128)}) %reduce-scatter.22.cloned.1.call-update) | async-done | bytes 73744 | tf_op jit(solution)/shard_map/reduce_scatter | solution.py:208
  1191.2 143.0 %reduce-scatter.26.cloned.1.call-done = f32[1536,48]{0,1:T(8,128)} async-done(((f32[1536,768]{0,1:T(8,128)}), f32[1536,48]{0,1:T(8,128)}) %reduce-scatter.26.cloned.1.call-update) | async-done | bytes 294928 | tf_op jit(solution)/shard_map/reduce_scatter | solution.py:205
  1334.2 143.4 %reduce-scatter.24.cloned.1.call-done = f32[48,1536]{1,0:T(8,128)} async-done(((f32[768,1536]{1,0:T(8,128)}), f32[48,1536]{1,0:T(8,128)}) %reduce-scatter.24.cloned.1.call-update) | async-done | bytes 294928 | tf_op jit(solution)/shard_map/reduce_scatter | solution.py:204
  (682 shorter events, 322.2 us)
Async XLA Ops:
  7.2 99.1 %copy-start.120 = (bf16[48,384]{1,0:T(8,128)(2,1)S(1)}, bf16[48,384]{1,0:T(8,128)(2,1)}, u32[]{:S(2)}) copy-start(bf16[48,384]{1,0:T(8,128)(2,1)} %param.16) | copy-start | bytes 110596
  7.3 140.3 %copy-start.121 = (bf16[48,384]{1,0:T(8,128)(2,1)S(1)}, bf16[48,384]{1,0:T(8,128)(2,1)}, u32[]{:S(2)}) copy-start(bf16[48,384]{1,0:T(8,128)(2,1)} %param.17) | copy-start | bytes 110596
  7.3 184.7 %all-gather.7.cloned.1.call-start = ((), (), s32[]{:S(2)}) async-start(), calls=%async_computation.11 | async-start | bytes 4718592 | tf_op jit(solution)/shard_map/all_gather | solution.py:129
  8.0 293.4 %all-gather.9.cloned.1.call-start = ((), (), s32[]{:S(2)}) async-start(), calls=%async_computation.12 | async-start | bytes 1216512 | tf_op jit(solution)/shard_map/all_gather | solution.py:118
  8.7 302.8 %all-gather.13.cloned.1.call-start = ((), (), s32[]{:S(2)}) async-start(), calls=%async_computation.14 | async-start | bytes 2506752 | tf_op jit(solution)/shard_map/all_gather | solution.py:114
  62.4 151.5 %copy-start.102 = (pred[2,1024]{1,0:T(4,128)(4,1)}, pred[2,1024]{1,0:T(4,128)(4,1)S(1)}, u32[]{:S(2)}) copy-start(pred[2,1024]{1,0:T(4,128)(4,1)S(1)} %get-tuple-element.190) | copy-start | bytes 6148
  62.4 204.7 %copy-start.94 = (f32[2,1024]{1,0:T(2,128)}, f32[2,1024]{1,0:T(2,128)S(1)}, u32[]{:S(2)}) copy-start(f32[2,1024]{1,0:T(2,128)S(1)} %get-tuple-element.191) | copy-start | bytes 24580
  297.6 6.2 all-to-all-start
  301.3 17.8 %all-gather.11.cloned.1.call-start = ((), (), s32[]{:S(2)}) async-start(), calls=%async_computation.13 | async-start | bytes 4718592 | tf_op jit(solution)/shard_map/all_gather | solution.py:155
  310.9 74.2 %all-gather.15.cloned.1.call-start = ((), (), s32[]{:S(2)}) async-start(), calls=%async_computation.15 | async-start | bytes 2506752 | tf_op jit(solution)/shard_map/all_gather | solution.py:115
  311.5 92.2 %reduce-scatter.16.cloned.1.call-start = ((), (), s32[]{:S(2)}) async-start(), calls=%async_computation.16 | async-start | bytes 4718592 | tf_op jit(solution)/shard_map/reduce_scatter | solution.py:159
  394.2 34.4 %all-gather.17.cloned.1.call-start = ((), (), s32[]{:S(2)}) async-start(), calls=%async_computation.17 | async-start | bytes 4718592 | tf_op jit(solution)/shard_map/all_gather | solution.py:165
  415.1 52.3 %reduce-scatter.18.cloned.1.call-start = ((), (), s32[]{:S(2)}) async-start(), calls=%async_computation.18 | async-start | bytes 4718592 | tf_op jit(solution)/shard_map/reduce_scatter | solution.py:177
  455.1 366.3 %reduce-scatter.20.cloned.1.call-start = ((), (), s32[]{:S(2)}) async-start(), calls=%async_computation.19 | async-start | bytes 4718592 | tf_op jit(solution)/shard_map/reduce_scatter | solution.py:194
  684.1 144.0 %reduce-scatter.28.cloned.1.call-start = ((), (), s32[]{:S(2)}) async-start(), calls=%async_computation.23 | async-start | bytes 1253376
  691.7 265.9 %reduce-scatter.30.cloned.1.call-start = ((), (), s32[]{:S(2)}) async-start(), calls=%async_computation.24 | async-start | bytes 1253376
  699.4 387.3 %reduce-scatter.32.cloned.1.call-start = ((), (), s32[]{:S(2)}) async-start(), calls=%async_computation.25 | async-start | bytes 1253376
  706.9 484.3 %reduce-scatter.22.cloned.1.call-start = ((), (), s32[]{:S(2)}) async-start(), calls=%async_computation.20 | async-start | bytes 2433024 | tf_op jit(solution)/shard_map/reduce_scatter | solution.py:208
  712.2 622.0 %reduce-scatter.26.cloned.1.call-start = ((), (), s32[]{:S(2)}) async-start(), calls=%async_computation.22 | async-start | bytes 5013504 | tf_op jit(solution)/shard_map/reduce_scatter | solution.py:205
  721.9 755.7 %reduce-scatter.24.cloned.1.call-start = ((), (), s32[]{:S(2)}) async-start(), calls=%async_computation.21 | async-start | bytes 5013504 | tf_op jit(solution)/shard_map/reduce_scatter | solution.py:204
  763.3 3.8 collective-permute-start
  767.2 3.8 collective-permute-start.1
  771.1 4.5 collective-permute-start.2
  775.7 45.0 %collective-permute-start.3 = (f32[6,33]{0,1:T(8,128)S(1)}, f32[6,33]{0,1:T(8,128)S(1)}, u32[]{:S(2)}, u32[]{:S(2)}) collective-permute-start(f32[6,33]{0,1:T(8,128)S(1)} %add.381), channel_id=1, source_target_pairs={{0,16},{2,18},{4,20},{6,22},{8,24},{10,26},{12,28},{14,30},{16,0},... | collective-permute-start | bytes 2384 | tf_op jit(solution)/shard_map/ppermute | solution.py:216
  (213 other events, 1686.7 us)
Sparse Core Ops, SparseCore 0:
  9.6 14.8 all-gather.6
  27.4 56.5 all-gather.8
  86.7 69.0 all-gather.12
  311.0 8.0 all-gather.10
  321.7 63.3 all-gather.14
  394.3 9.3 reduce-scatter.15
  415.2 13.3 all-gather.16
  455.2 12.1 reduce-scatter.17
  684.2 12.2 reduce-scatter.19
  701.7 126.4 reduce-scatter.27
  833.5 124.0 reduce-scatter.29
  962.7 123.9 reduce-scatter.31
  1092.6 98.5 reduce-scatter.21
  1196.8 137.3 reduce-scatter.25
  1339.8 137.7 reduce-scatter.23
